TPU v7x, 512 devices: a 8x2x16 block of a 8x8x16 slice. The times are simulated.
512 devices in a mesh: groups: 2 (over y), expert: 32 (over z, core), tensor: 8 (over x).
Axes of the slice: x: 8, y: 2, z: 16, core: 2. Of those that a mesh axis runs over, the one named last changes fastest.
The devices are a block of a 8x8x16 slice.
Arguments:
- queries: bfloat16 [2048, 4096], P(('groups', 'expert')), parts along dimension 0, may hold values from -200 to 200
- own_kv: bfloat16 [2048, 1024], P(('groups', 'expert')), parts along dimension 0, may hold values from -6 to 6
- prompt_cache: bfloat16 [64, 256, 1024], P(('groups', 'expert'), 'tensor'), parts along dimension 0, may hold values from -8 to 8
- prompt_len: int32 [64], P(('groups', 'expert')), parts along dimension 0, may hold values from 2 to 256
- token_prompt: int32 [2048], P(('groups', 'expert')), parts along dimension 0, may hold values from 0 to 31, as said below
- residual: bfloat16 [2048, 2048], P(('groups', 'expert')), parts along dimension 0, may hold values from -3 to 3
- out_weight: bfloat16 [4096, 2048], P('tensor', 'expert'), may hold values from -0.1875 to 0.1875
- route_ids: int32 [2048, 8], P(('groups', 'expert')), parts along dimension 0, may hold values from 0 to 63, all different within a row; in each aligned block of 32 rows (0 to 31, 32 to 63, ...) at most 6 rows name the same one
- route_weights: float32 [2048, 8], P(('groups', 'expert')), parts along dimension 0, may hold values from 0.05 to 0.3
- w_gate: bfloat16 [64, 2048, 1024], P('expert', None, 'tensor'), may hold values from -0.125 to 0.125
- w_up: bfloat16 [64, 2048, 1024], P('expert', None, 'tensor'), may hold values from -0.125 to 0.125
- w_down: bfloat16 [64, 1024, 2048], P('expert', 'tensor'), may hold values from -0.25 to 0.25
Outputs:
- mixed: bfloat16 [2048, 2048], P(('groups', 'expert'), 'tensor'), parts along dimension 0
There are 2 independent parts, one for each index of `groups`. A program takes and returns all parts, laid end to end along the dimension named above; an argument that names none is the same for every part. Nothing has to cross between parts.
Inputs may be any that keep to these rules, and one draw needn't show every extreme that they name: `token_prompt`: each index of the expert axis holds 2 tokens of each of 16 prompts and none of the others; each prompt has tokens on exactly 16 indices. `route_ids`: A row names distinct experts. Within the 32 rows of one index of the expert axis no expert is named more than 6 times, and in some of these blocks one is named exactly 6 times.
All inputs are finite; a program needn't handle non-finite values.
Results may differ from a plain program's by a relative error of at most 0.015.
Values may be sent and summed in bfloat16 or wider, within the bound.
No kernel may reach another device: no remote copies, remote signals or barrier semaphores. Data moves between devices by JAX's collectives and lax.ppermute only.
A program may use at most 64 MiB of HBM per device.

v0:
```python
import jax
import jax.numpy as jnp
from jax import lax
from jax.sharding import Mesh
from jax.sharding import PartitionSpec as P

HD = 128
EXPERT = ("expert_0", "expert_1")
GROUPS_EXPERT = ("groups", "expert_0", "expert_1")
MASKED_SCORE = -1e30


def combined_all(x, axis, combine):
    everything = jax.tree.map(
        lambda part, kind: lax.all_gather(part.astype(kind), axis),
        x,
        jax.tree.map(lambda a: jnp.bfloat16 if a.dtype == jnp.float32 else a.dtype, x),
    )

    def take(k):
        return jax.tree.map(lambda part, own: part[k].astype(own.dtype), everything, x)

    return lax.fori_loop(
        1, lax.axis_size(axis), lambda k, so_far: combine(so_far, take(k)), take(0)
    )


def sent_to_all(x, axis):
    copies = jnp.broadcast_to(x, (lax.axis_size(axis), *x.shape))
    return lax.all_to_all(copies, axis, split_axis=0, concat_axis=0, tiled=True)


def joined_along(tiles, dim):
    tiles = jnp.moveaxis(tiles, 0, dim)
    shape = tiles.shape
    return tiles.reshape(*shape[:dim], shape[dim] * shape[dim + 1], *shape[dim + 2 :])


def gathered_copies(x, axis, dim):
    tiles = sent_to_all(x, axis)
    return joined_along(tiles, dim)


def in_blocks(x, dim, length):
    shape = x.shape
    tiles = x.reshape(*shape[:dim], length, shape[dim] // length, *shape[dim + 1 :])
    return jnp.moveaxis(tiles, dim, 0)


def exchange_in_order(tiles, axes, sequence):
    shape = [lax.axis_size(a) for a in axes]
    tiles = tiles.reshape(*shape, *tiles.shape[1:])
    for k in sequence:
        tiles = lax.all_to_all(tiles, axes[k], split_axis=k, concat_axis=k, tiled=True)
    return tiles.reshape(-1, *tiles.shape[len(axes) :])


def two_step_exchange(x, groups, sequence, split_dim, concat_dim):
    length = lax.axis_size(groups[0]) * lax.axis_size(groups[1])
    tiles = in_blocks(x, split_dim, length)
    return joined_along(exchange_in_order(tiles, groups, sequence), concat_dim)


def sent_and_summed(x, axis, dim):
    tiles = in_blocks(x, dim, lax.axis_size(axis))
    arrived = lax.all_to_all(tiles, axis, split_axis=0, concat_axis=0, tiled=True)
    return arrived.astype(jnp.float32).sum(axis=0)


def combine_parts(earlier, later):
    top_a, sum_a, value_a = earlier
    top_b, sum_b, value_b = later
    top_score = jnp.maximum(top_a, top_b)
    shrink_a = jnp.exp(top_a - top_score)
    shrink_b = jnp.exp(top_b - top_score)
    return (
        top_score,
        sum_a * shrink_a + sum_b * shrink_b,
        value_a * shrink_a[..., None] + value_b * shrink_b[..., None],
    )


def local(
    queries,
    own_kv,
    prompt_cache,
    prompt_len,
    token_prompt,
    residual,
    out_weight,
    route_ids,
    route_weights,
    w_gate,
    w_up,
    w_down,
):
    tokens = queries.shape[0]
    half_cols = own_kv.shape[1] // 2
    kv_heads = half_cols // HD
    head_count = queries.shape[1] // HD
    group_size = head_count // kv_heads
    score_scale = HD ** (-0.5)
    expert_groups = lax.axis_size(EXPERT)
    fan_count = expert_groups // 2
    per_prompt = tokens // fan_count
    order = jnp.argsort(token_prompt, stable=True)
    inverse = jnp.argsort(order)
    held_prompts = token_prompt[order].reshape(fan_count, per_prompt)[:, 0]
    sorted_query = queries[order].reshape(fan_count, per_prompt, kv_heads, group_size, HD)
    sorted_own = own_kv[order]
    own_keys = sorted_own[:, :half_cols].reshape(fan_count, per_prompt, kv_heads, HD)
    own_values = (
        sorted_own[:, half_cols:].reshape(fan_count, per_prompt, kv_heads, HD).astype(jnp.float32)
    )
    own_score = (
        jnp.einsum("imgjd,imgd->imgj", sorted_query, own_keys, preferred_element_type=jnp.float32)
        * score_scale
    )
    tensor_pos = lax.axis_index("tensor")
    leading = tensor_pos == 0
    start_top = jnp.where(leading, own_score, MASKED_SCORE)
    start_sum = jnp.where(leading, jnp.ones_like(own_score), jnp.zeros_like(own_score))
    start_values = jnp.where(
        leading,
        jnp.broadcast_to(
            own_values[:, :, :, None, :], (fan_count, per_prompt, kv_heads, group_size, HD)
        ),
        0.0,
    )
    block_len = prompt_cache.shape[1]
    positions = tensor_pos * block_len + jnp.arange(block_len, dtype=jnp.int32)
    cache_piece = lax.all_gather(prompt_cache, EXPERT, axis=0, tiled=True)
    length_piece = lax.all_gather(prompt_len, EXPERT, axis=0, tiled=True)
    shard_count = cache_piece.shape[0]
    owners = jnp.arange(shard_count, dtype=jnp.int32)
    matched = owners[:, None] == held_prompts[None, :]
    match_half = matched.astype(jnp.bfloat16)
    match_full = matched.astype(jnp.float32)
    present = jnp.any(matched, 0)
    piece_query = jnp.einsum(
        "qi,imgjd->qmgjd", match_half, sorted_query, preferred_element_type=jnp.float32
    ).astype(jnp.bfloat16)
    key_rows = cache_piece[:, :, :half_cols].reshape(shard_count, block_len, kv_heads, HD)
    value_rows = (
        cache_piece[:, :, half_cols:]
        .reshape(shard_count, block_len, kv_heads, HD)
        .astype(jnp.float32)
    )
    inside = (positions[None, :] < length_piece[:, None])[:, None, None, None, :]
    score_rows = (
        jnp.einsum("qmgjd,qpgd->qmgjp", piece_query, key_rows, preferred_element_type=jnp.float32)
        * score_scale
    )
    score_rows = jnp.where(inside, score_rows, MASKED_SCORE)
    piece_top = jnp.max(score_rows, -1)
    weights = jnp.where(inside, jnp.exp(score_rows - piece_top[..., None]), 0.0)
    piece_sum = jnp.sum(weights, -1)
    piece_values = jnp.einsum("qmgjp,qpgd->qmgjd", weights, value_rows)
    group_top = jnp.einsum("qi,qmgj->imgj", match_full, piece_top)
    group_top = jnp.where(present[:, None, None, None], group_top, MASKED_SCORE)
    group_sum = jnp.einsum("qi,qmgj->imgj", match_full, piece_sum)
    group_values = jnp.einsum("qi,qmgjd->imgjd", match_full, piece_values)
    folded = combine_parts(
        (start_top, start_sum, start_values), (group_top, group_sum, group_values)
    )
    top_score, weight_sum, value_sum = combined_all(folded, "tensor", combine_parts)
    attn_sorted = (value_sum / weight_sum[..., None]).reshape(tokens, head_count * HD)
    attn = attn_sorted[inverse].astype(jnp.bfloat16)
    rows_here = out_weight.shape[0]
    attn_mine = lax.dynamic_slice_in_dim(attn, tensor_pos * rows_here, rows_here, 1)
    column_terms = jnp.dot(
        gathered_copies(attn_mine, EXPERT, 0), out_weight, preferred_element_type=jnp.float32
    )
    partials = two_step_exchange(
        column_terms.astype(jnp.bfloat16), ("expert_0", "expert_1"), (1, 0), 0, 1
    ).astype(column_terms.dtype)
    model_width = residual.shape[1]
    col_width = model_width // lax.axis_size("tensor")
    col_start = tensor_pos * col_width
    resid_cols = lax.dynamic_slice_in_dim(residual, col_start, col_width, 1)
    experts_here = w_gate.shape[0]
    experts = experts_here * expert_groups
    picks = route_ids.shape[1]
    capacity = min(tokens, 3 * tokens * picks // (2 * experts))
    flat_ids = route_ids.reshape(-1)
    expert_marks = (flat_ids[:, None] == jnp.arange(experts, dtype=jnp.int32)[None, :]).astype(
        jnp.int32
    )
    slot_index = jnp.sum((jnp.cumsum(expert_marks, 0) - expert_marks) * expert_marks, 1)
    destination = flat_ids * capacity + slot_index
    source_rows = jnp.arange(tokens * picks, dtype=jnp.int32) // picks
    head_total = sent_and_summed(partials.astype(jnp.bfloat16), "tensor", 1)
    hidden_cols = (resid_cols.astype(jnp.float32) + head_total).astype(jnp.bfloat16)
    outgoing = (
        jnp.zeros((experts * capacity, col_width), jnp.bfloat16)
        .at[destination]
        .set(hidden_cols[source_rows])
    )
    outgoing = outgoing.reshape(expert_groups, experts_here, capacity, col_width)
    arrived = lax.all_to_all(outgoing, EXPERT, split_axis=0, concat_axis=0, tiled=True)
    arrived = gathered_copies(arrived, "tensor", 3)
    gate_proj = jnp.einsum("sxcd,xdf->sxcf", arrived, w_gate, preferred_element_type=jnp.float32)
    up_proj = jnp.einsum("sxcd,xdf->sxcf", arrived, w_up, preferred_element_type=jnp.float32)
    activated = (jax.nn.silu(gate_proj) * up_proj).astype(jnp.bfloat16)
    expert_partials = jnp.einsum(
        "sxcf,xfd->sxcd", activated, w_down, preferred_element_type=jnp.float32
    )
    summed = sent_and_summed(expert_partials.astype(jnp.bfloat16), "tensor", 3).astype(jnp.bfloat16)
    returned = lax.all_to_all(summed, EXPERT, split_axis=0, concat_axis=0, tiled=True).reshape(
        experts * capacity, col_width
    )
    picked = returned[destination].reshape(tokens, picks, col_width).astype(jnp.float32)
    expert_mix = jnp.sum(route_weights[:, :, None] * picked, 1)
    return (hidden_cols.astype(jnp.float32) + expert_mix).astype(jnp.bfloat16)


def solution(mesh):
    split = Mesh(
        mesh.devices.reshape(mesh.shape["groups"], 16, 2, mesh.shape["tensor"]),
        ("groups", "expert_0", "expert_1", "tensor"),
    )
    return jax.shard_map(
        local,
        mesh=split,
        in_specs=(
            P(GROUPS_EXPERT, None),
            P(GROUPS_EXPERT, None),
            P(GROUPS_EXPERT, "tensor", None),
            P(GROUPS_EXPERT),
            P(GROUPS_EXPERT),
            P(GROUPS_EXPERT, None),
            P("tensor", EXPERT),
            P(GROUPS_EXPERT, None),
            P(GROUPS_EXPERT, None),
            P(EXPERT, None, "tensor"),
            P(EXPERT, None, "tensor"),
            P(EXPERT, "tensor", None),
        ),
        out_specs=P(GROUPS_EXPERT, "tensor"),
        check_vma=False,
    )
```

profile of v0, /device:TPU:65, one launch (start us, length us, event | category | flops | bytes accessed | tf_op | source)
XLA Modules:
  0.0 455.3 jit_solution(9609944883478127839)
XLA Ops:
  6.6 0.7 all-gather.6.cloned.1.call-update
  7.4 2.3 sort.34
  9.7 1.6 sort.35
  11.3 1.4 gather_fusion.2
  12.6 0.7 gather_fusion
  14.2 0.6 gather_fusion.1
  15.3 1.3 dynamic-slice
  16.6 0.8 dynamic-update-slice
  17.3 57.1 %all-reduce = s32[32]{0:T(128)S(1)} all-reduce(s32[32]{0:T(128)S(1)} %dynamic-update-slice), channel_id=1, replica_groups=mesh['groups'=2,'expert_0'=16,'expert_1'=2,'tensor'=8] {'expert_0','expe..., use_global_device_ids=true, to_apply=%add | all-reduce | flops 32 | bytes 256
  74.8 1.2 convolution_convert_fusion.1
  76.0 42.0 %all-gather.6.cloned.1.call-done = bf16[32,32,1024]{2,1,0:T(8,128)(2,1)} async-done(((bf16[1,32,1024]{2,1,0:T(8,128)(2,1)}), bf16[32,32,1024]{2,1,0:T(8,128)(2,1)}) %all-gather.6.cloned.1.call-update) | async-done | bytes 2097168 | tf_op jit(solution)/shard_map/all_gather | solution.py:132
  118.1 2.7 fusion.51
  121.1 1.9 fusion.52
  123.2 0.8 fusion.16
  124.3 1.1 reshape.195
  125.4 1.7 convolution_bitcast_fusion
  127.2 1.3 fusion.6
  128.6 20.8 %all-gather = bf16[128,2,4,8]{3,2,1,0:T(4,128)(2,1)S(1)} all-gather(bf16[16,2,4,8]{3,2,1,0:T(4,128)(2,1)S(1)} %copy.80), channel_id=2, replica_groups=mesh['groups'=2,'expert_0'=16,'expert_1'=2,'tensor'=8] {'tensor'}, dimensions={0}, use_global_device_ids=true | all-gather | bytes 18432 | tf_op jit(solution)/shard_map/all_gather | solution.py:15
  149.6 21.1 %all-gather.1 = bf16[128,2,4,8]{3,2,1,0:T(4,128)(2,1)S(1)} all-gather(bf16[16,2,4,8]{3,2,1,0:T(4,128)(2,1)S(1)} %copy.82), channel_id=3, replica_groups=mesh['groups'=2,'expert_0'=16,'expert_1'=2,'tensor'=8] {'tensor'}, dimensions={0}, use_global_device_ids=true | all-gather | bytes 18432 | tf_op jit(solution)/shard_map/all_gather | solution.py:15
  171.3 4.4 all-gather.8.cloned.1.call-done
  175.7 1.0 slice_convert_fusion
  176.8 11.6 %while.19 = (s32[]{:T(128)}, f32[16,2,4,8]{0,3,2,1:T(8,128)S(1)}, f32[16,2,4,8]{0,3,2,1:T(8,128)S(1)}, f32[16,2,4,8,128]{4,3,2,1,0:T(8,128)S(1)}, bf16[8,16,2,4,...) while((s32[]{:T(128)}, f32[16,2,4,8]{0,3,2,1:T(8,128)S(1)}, ...), condition=%wide.region_5.6_spmd, body=%wide.region_4.5_spmd.sunk | while | flops 532485 | bytes 1888407 | solution.py:23
  176.9 1.0 constant_dynamic-slice_fusion.2
  178.1 0.4 fusion.65
  178.6 1.0 constant_dynamic-slice_fusion.2
  179.8 0.4 fusion.65
  180.2 1.0 constant_dynamic-slice_fusion.2
  181.4 0.4 fusion.65
  181.9 1.0 constant_dynamic-slice_fusion.2
  183.1 0.4 fusion.65
  183.5 1.0 constant_dynamic-slice_fusion.2
  184.7 0.4 fusion.65
  185.2 1.0 constant_dynamic-slice_fusion.2
  186.4 0.4 fusion.65
  186.9 1.0 constant_dynamic-slice_fusion.2
  188.1 0.4 fusion.65
  188.9 0.7 gather_fusion.3
  189.7 1.1 broadcast_in_dim.93
  190.8 18.3 %all-to-all-start = ((bf16[32,32,512]{2,1,0:T(8,128)(2,1)}), bf16[32,32,512]{2,1,0:T(8,128)(2,1)S(1)}, u32[]{:S(2)}, u32[]{:S(2)}) async-start(bf16[32,32,512]{2,1,0:T(8,128)(2,1)} %broadcast_in_dim.93), calls=%async_computation | async-start | bytes 2097152 | tf_op jit(solution)/shard_map/all_to_all | solution.py:30
  209.3 0.6 reduce-window.6
  209.9 54.7 %all-to-all-done = bf16[32,32,512]{2,1,0:T(8,128)(2,1)S(1)} async-done(((bf16[32,32,512]{2,1,0:T(8,128)(2,1)}), bf16[32,32,512]{2,1,0:T(8,128)(2,1)S(1)}, u32[]{:S(2)}, u32[]{:S(2)}) %all-to-all-start) | async-done | bytes 1048608 | tf_op jit(solution)/shard_map/all_to_all | solution.py:30
  264.6 0.4 convolution_convert_fusion.2
  265.5 4.0 all_to_all.40
  269.7 0.9 reshape.313
  270.6 4.1 all-to-all-start.2
  275.2 11.5 %all-to-all-done.2 = bf16[16,2,2048]{2,1,0:T(2,128)(2,1)S(1)} async-done(((bf16[16,2,2048]{2,1,0:T(2,128)(2,1)}), bf16[16,2,2048]{2,1,0:T(2,128)(2,1)S(1)}, u32[]{:S(2)}, u32[]{:S(2)}) %all-to-all-start.2) | async-done | bytes 131104 | tf_op jit(solution)/shard_map/all_to_all | solution.py:54
  287.2 0.7 copy.97
  287.9 4.0 all-to-all-start.3
  292.0 7.8 %all-to-all-done.3 = bf16[8,32,256]{2,1,0:T(8,128)(2,1)S(1)} async-done(((bf16[8,32,256]{2,1,0:T(8,128)(2,1)}), bf16[8,32,256]{2,1,0:T(8,128)(2,1)S(1)}, u32[]{:S(2)}, u32[]{:S(2)}) %all-to-all-start.3) | async-done | bytes 131104 | tf_op jit(solution)/shard_map/all_to_all | solution.py:66
  299.9 0.7 add_convert_fusion.1
  300.6 2.2 scatter_custom_fusion
  303.1 27.2 %all_to_all.41 = bf16[32,2,6,256]{3,1,2,0:T(2,128)(2,1)S(1)} all-to-all(bf16[32,2,6,256]{3,1,2,0:T(2,128)(2,1)S(1)} %copy.103), channel_id=1, replica_groups=mesh['groups'=2,'expert_0'=16,'expert_1'=2,'tensor'=8] {'expert_0','expe..., dimensions={0} | all-to-all | bytes 393216 | tf_op jit(solution)/shard_map/all_to_all | solution.py:200
  330.5 40.4 %all_to_all.42 = bf16[8,32,2,6,256]{4,1,3,2,0:T(8,128)(2,1)S(1)} all-to-all(bf16[8,32,2,6,256]{4,1,3,2,0:T(8,128)(2,1)S(1)} %broadcast_in_dim.95), channel_id=1, replica_groups=mesh['groups'=2,'expert_0'=16,'expert_1'=2,'tensor'=8] {'tensor'}, dimensions={0} | all-to-all | bytes 3145728 | tf_op jit(solution)/shard_map/all_to_all | solution.py:30
  371.1 1.0 copy-done.4
  372.1 0.6 convolution_bitcast_fusion.2
  372.7 3.3 convolution_convert_fusion
  376.1 1.6 copy.148
  377.7 40.0 %all_to_all.43 = bf16[8,32,2,6,256]{4,1,3,2,0:T(8,128)(2,1)S(1)} all-to-all(bf16[8,32,2,6,256]{4,1,3,2,0:T(8,128)(2,1)S(1)} %bitcast.142), channel_id=1, replica_groups=mesh['groups'=2,'expert_0'=16,'expert_1'=2,'tensor'=8] {'tensor'}, dimensions={0} | all-to-all | bytes 3145728 | tf_op jit(solution)/shard_map/all_to_all | solution.py:66
  417.7 0.3 reduce_sum.54
  418.0 0.9 copy.108
  418.9 9.0 %all-to-all-start.7 = ((bf16[32,2,6,256]{3,1,2,0:T(2,128)(2,1)}), bf16[32,2,6,256]{3,1,2,0:T(2,128)(2,1)S(1)}, u32[]{:S(2)}, u32[]{:S(2)}) async-start(bf16[32,2,6,256]{3,1,2,0:T(2,128)(2,1)} %copy.108), calls=%async_computation.7 | async-start | bytes 393216 | tf_op jit(solution)/shard_map/all_to_all | solution.py:209
  428.0 18.4 %all-to-all-done.7 = bf16[32,2,6,256]{3,1,2,0:T(2,128)(2,1)S(1)} async-done(((bf16[32,2,6,256]{3,1,2,0:T(2,128)(2,1)}), bf16[32,2,6,256]{3,1,2,0:T(2,128)(2,1)S(1)}, u32[]{:S(2)}, u32[]{:S(2)}) %all-to-all-start.7) | async-done | bytes 196640 | tf_op jit(solution)/shard_map/all_to_all | solution.py:209
  446.5 1.2 gather_fusion.4
  447.8 0.6 add_convert_fusion
  (111 shorter events, 8.0 us)
Async XLA Ops:
  6.5 366.2 %copy-start = (bf16[2,128,2048]{2,1,0:T(8,128)(2,1)S(1)}, bf16[2,128,2048]{2,1,0:T(8,128)(2,1)}, u32[]{:S(2)}) copy-start(bf16[2,128,2048]{2,1,0:T(8,128)(2,1)} %param.25) | copy-start | bytes 3145732
  6.6 6.1 %copy-start.1 = (bf16[32,4096]{1,0:T(8,128)(2,1)S(1)}, bf16[32,4096]{1,0:T(8,128)(2,1)}, u32[]{:S(2)}) copy-start(bf16[32,4096]{1,0:T(8,128)(2,1)} %param.14) | copy-start | bytes 786436
  6.6 111.5 %all-gather.6.cloned.1.call-start = ((), (), s32[]{:S(2)}) async-start(), calls=%async_computation.8 | async-start | bytes 2162688 | tf_op jit(solution)/shard_map/all_gather | solution.py:132
  7.3 168.4 %all-gather.8.cloned.1.call-start = ((), (), s32[]{:S(2)}) async-start(), calls=%async_computation.9 | async-start | bytes 2359296 | tf_op jit(solution)/shard_map/all_gather | solution.py:15
  12.6 1.5 copy-start.2
  122.9 1.4 copy-start.3
  189.7 19.4 %copy-start.6 = (s32[32,8]{0,1:T(8,128)S(1)}, s32[32,8]{0,1:T(8,128)}, u32[]{:S(2)}) copy-start(s32[32,8]{0,1:T(8,128)} %param.21) | copy-start | bytes 3076
  189.7 74.9 %copy-start.5 = (bf16[512,64]{0,1:T(8,128)(2,1)S(1)}, bf16[512,64]{0,1:T(8,128)(2,1)}, u32[]{:S(2)}) copy-start(bf16[512,64]{0,1:T(8,128)(2,1)} %param.20) | copy-start | bytes 196612
  190.8 73.8 %all-to-all-start = ((bf16[32,32,512]{2,1,0:T(8,128)(2,1)}), bf16[32,32,512]{2,1,0:T(8,128)(2,1)S(1)}, u32[]{:S(2)}, u32[]{:S(2)}) async-start(bf16[32,32,512]{2,1,0:T(8,128)(2,1)} %broadcast_in_dim.93), calls=%async_computation | async-start | bytes 2097152 | tf_op jit(solution)/shard_map/all_to_all | solution.py:30
  270.6 16.0 %all-to-all-start.2 = ((bf16[16,2,2048]{2,1,0:T(2,128)(2,1)}), bf16[16,2,2048]{2,1,0:T(2,128)(2,1)S(1)}, u32[]{:S(2)}, u32[]{:S(2)}) async-start(bf16[16,2,2048]{2,1,0:T(2,128)(2,1)} %reshape.313), calls=%async_computation.2 | async-start | bytes 262144 | tf_op jit(solution)/shard_map/all_to_all | solution.py:54
  287.9 12.0 %all-to-all-start.3 = ((bf16[8,32,256]{2,1,0:T(8,128)(2,1)}), bf16[8,32,256]{2,1,0:T(8,128)(2,1)S(1)}, u32[]{:S(2)}, u32[]{:S(2)}) async-start(bf16[8,32,256]{2,1,0:T(8,128)(2,1)} %copy.97), calls=%async_computation.3 | async-start | bytes 262144 | tf_op jit(solution)/shard_map/all_to_all | solution.py:66
  370.9 1.2 copy-start.4
  417.7 10.2 %copy-start.7 = (f32[32,8]{0,1:T(8,128)S(1)}, f32[32,8]{0,1:T(8,128)}, u32[]{:S(2)}) copy-start(f32[32,8]{0,1:T(8,128)} %param.22) | copy-start | bytes 3076
  418.9 27.5 %all-to-all-start.7 = ((bf16[32,2,6,256]{3,1,2,0:T(2,128)(2,1)}), bf16[32,2,6,256]{3,1,2,0:T(2,128)(2,1)S(1)}, u32[]{:S(2)}, u32[]{:S(2)}) async-start(bf16[32,2,6,256]{3,1,2,0:T(2,128)(2,1)} %copy.108), calls=%async_computation.7 | async-start | bytes 393216 | tf_op jit(solution)/shard_map/all_to_all | solution.py:209
Sparse Core Ops, SparseCore 0:
  9.5 108.5 all-gather.5
  128.6 46.9 all-gather.7
where the time goes:
time: 457 us; the launch traced here: 455 us
  blocking collectives  211 us (46%)
  waiting for transfers between devices  140 us (31%)
  starting transfers between devices  35.4 us (8%)
  local copies, waits for them, and re-layouts  31.7 us (7%)
  between operations  14.6 us (3%)
  other arithmetic  11.9 us (3%)
  matrix products  11.1 us (2%)
    unnamed x1, blocking collectives  57.1 us
    all_to_all x1, waiting for transfers between devices, sent_to_all(): return lax.all_to_all(copies, axis, split_axis=0, concat_axis=0, tiled=True)  54.7 us
    all_gather x1, waiting for transfers between devices, local(): cache_piece = lax.all_gather(prompt_cache, EXPERT, axis=0, tiled=True)  42 us
    all_gather x2, blocking collectives, combined_all(): lax.all_gather(part.astype(kind), axis)  41.9 us
    all_to_all x1, blocking collectives, sent_to_all(): return lax.all_to_all(copies, axis, split_axis=0, concat_axis=0, tiled=True)  40.4 us
    all_to_all x1, blocking collectives, sent_and_summed(): lax.all_to_all(tiles, axis, split_axis=0, concat_axis=0, tiled=True)  40 us
    all_to_all x1, blocking collectives, local(): lax.all_to_all(outgoing, EXPERT, split_axis=0, concat_axis=0, tiled=True)  27.2 us
    all_to_all x1, waiting for transfers between devices, local(): lax.all_to_all(summed, EXPERT, split_axis=0, concat_axis=0, tiled=True)  18.4 us
  transfers between devices with their start and end apart: 6, of which 6 were waited for; matrix products, arithmetic and copies ran while one was open for 3% of the time, Pallas kernels for 0%

commit v1 on v0

--- a/solution.py
+++ b/solution.py
@@ -129,7 +129,9 @@
     )
     block_len = prompt_cache.shape[1]
     positions = tensor_pos * block_len + jnp.arange(block_len, dtype=jnp.int32)
-    cache_piece = lax.all_gather(prompt_cache, EXPERT, axis=0, tiled=True)
+    cache_piece = jnp.concatenate(
+        lax.all_to_all(jnp.stack([prompt_cache] * lax.axis_size(EXPERT)), EXPERT, 0, 0), axis=0
+    )
     length_piece = lax.all_gather(prompt_len, EXPERT, axis=0, tiled=True)
     shard_count = cache_piece.shape[0]
     owners = jnp.arange(shard_count, dtype=jnp.int32)

time: 457 us -> 505 us (1.11)
  starting transfers between devices: 35.4 us -> 80.5 us
  waiting for transfers between devices: 140 us -> 105 us
  blocking collectives: 211 us -> 240 us
  local copies, waits for them, and re-layouts: 31.7 us -> 38.2 us
    all_to_all x0 -> x1, starting transfers between devices: none -> 45.5 us  [local(): lax.all_to_all(jnp.stack([prompt_cache] * lax.axis_size(EXPERT)), EXPERT,...]
    all_gather x1 -> x0, waiting for transfers between devices: 42 us -> none  [local(): cache_piece = lax.all_gather(prompt_cache, EXPERT, axis=0, tiled=True)]
    unnamed x1, blocking collectives: 57.1 us -> 88.6 us
    all_gather x1, waiting for transfers between devices: 4.4 us -> 13 us  [combined_all(): lax.all_gather(part.astype(kind), axis)]
  transfers between devices with their start and end apart: 6 -> 6, of which waited for: 6 -> 5; matrix products, arithmetic and copies ran while one was open for 3% -> 4% of each run, Pallas kernels for 0% -> 0%
where the time goes in v1:
time: 505 us; the launch traced here: 504 us
  blocking collectives  240 us (48%)
  waiting for transfers between devices  105 us (21%)
  starting transfers between devices  80.5 us (16%)
  local copies, waits for them, and re-layouts  38.2 us (8%)
  between operations  14.6 us (3%)
  matrix products  12.5 us (2%)
  other arithmetic  12 us (2%)
    unnamed x1, blocking collectives  88.6 us
    all_to_all x1, waiting for transfers between devices, sent_to_all(): return lax.all_to_all(copies, axis, split_axis=0, concat_axis=0, tiled=True)  54.7 us
    all_to_all x1, starting transfers between devices, local(): lax.all_to_all(jnp.stack([prompt_cache] * lax.axis_size(EXPERT)), EXPERT,...  45.5 us
    all_to_all x1, blocking collectives, sent_to_all(): return lax.all_to_all(copies, axis, split_axis=0, concat_axis=0, tiled=True)  40.4 us
    all_to_all x1, blocking collectives, sent_and_summed(): lax.all_to_all(tiles, axis, split_axis=0, concat_axis=0, tiled=True)  40 us
    all_gather x2, blocking collectives, combined_all(): lax.all_gather(part.astype(kind), axis)  39.8 us
    all_to_all x1, blocking collectives, local(): lax.all_to_all(outgoing, EXPERT, split_axis=0, concat_axis=0, tiled=True)  27.2 us
    all_to_all x1, waiting for transfers between devices, local(): lax.all_to_all(summed, EXPERT, split_axis=0, concat_axis=0, tiled=True)  18.4 us
  transfers between devices with their start and end apart: 6, of which 5 were waited for; matrix products, arithmetic and copies ran while one was open for 4% of the time, Pallas kernels for 0%

profile of v1, /device:TPU:65, one launch (start us, length us, event | category | flops | bytes accessed | tf_op | source)
XLA Modules:
  0.0 503.8 jit_solution(8630308862392381148)
XLA Ops:
  6.6 2.5 stack.2
  9.1 45.5 %all-to-all-start = ((bf16[32,1,32,1024]{3,2,1,0:T(8,128)(2,1)}), bf16[32,1,32,1024]{3,2,1,0:T(8,128)(2,1)S(1)}, u32[]{:S(2)}, u32[]{:S(2)}) async-start(bf16[32,1,32,1024]{3,2,1,0:T(8,128)(2,1)} %stack.2), calls=%async_computation | async-start | bytes 4194304 | tf_op jit(solution)/shard_map/all_to_all | solution.py:133
  54.7 1.6 sort.34
  56.3 1.6 sort.35
  57.9 0.7 gather_fusion.2
  58.6 1.4 gather_fusion
  60.0 1.0 copy.127
  61.8 0.6 gather_fusion.1
  62.4 0.6 reshape.309
  63.1 1.7 fusion.53
  64.8 0.9 copy.111
  65.7 0.8 convert_select_fusion
  66.5 0.6 select_n.114
  67.2 0.9 copy.83
  68.0 1.3 dynamic-slice
  69.3 0.8 dynamic-update-slice
  70.0 88.6 %all-reduce = s32[32]{0:T(128)S(1)} all-reduce(s32[32]{0:T(128)S(1)} %dynamic-update-slice), channel_id=1, replica_groups=mesh['groups'=2,'expert_0'=16,'expert_1'=2,'tensor'=8] {'expert_0','expe..., use_global_device_ids=true, to_apply=%add | all-reduce | flops 32 | bytes 256
  159.0 1.2 convolution_convert_fusion.1
  160.3 1.7 fusion.51
  161.9 1.3 reshape.201
  163.3 1.9 fusion.52
  165.4 0.8 fusion.16
  166.5 1.1 reshape.202
  167.7 1.7 convolution_bitcast_fusion
  169.4 1.3 fusion.6
  170.8 19.3 %all-gather = bf16[128,2,4,8]{3,2,1,0:T(4,128)(2,1)S(1)} all-gather(bf16[16,2,4,8]{3,2,1,0:T(4,128)(2,1)S(1)} %copy.80), channel_id=2, replica_groups=mesh['groups'=2,'expert_0'=16,'expert_1'=2,'tensor'=8] {'tensor'}, dimensions={0}, use_global_device_ids=true | all-gather | bytes 18432 | tf_op jit(solution)/shard_map/all_gather | solution.py:15
  190.3 20.6 %all-gather.1 = bf16[128,2,4,8]{3,2,1,0:T(4,128)(2,1)S(1)} all-gather(bf16[16,2,4,8]{3,2,1,0:T(4,128)(2,1)S(1)} %copy.82), channel_id=3, replica_groups=mesh['groups'=2,'expert_0'=16,'expert_1'=2,'tensor'=8] {'tensor'}, dimensions={0}, use_global_device_ids=true | all-gather | bytes 18432 | tf_op jit(solution)/shard_map/all_gather | solution.py:15
  211.4 13.0 %all-gather.5.cloned.1.call-done = bf16[128,2,4,8,128]{4,0,3,2,1:T(8,128)(2,1)} async-done(((bf16[16,2,4,8,128]{4,0,3,2,1:T(8,128)(2,1)}), bf16[128,2,4,8,128]{4,0,3,2,1:T(8,128)(2,1)}) %all-gather.5.cloned.1.call-update) | async-done | bytes 2097168 | tf_op jit(solution)/shard_map/all_gather | solution.py:15
  224.4 1.0 slice_convert_fusion
  225.6 11.6 %while.19 = (s32[]{:T(128)}, f32[16,2,4,8]{0,3,2,1:T(8,128)S(1)}, f32[16,2,4,8]{0,3,2,1:T(8,128)S(1)}, f32[16,2,4,8,128]{4,3,2,1,0:T(8,128)S(1)}, bf16[8,16,2,4,...) while((s32[]{:T(128)}, f32[16,2,4,8]{0,3,2,1:T(8,128)S(1)}, ...), condition=%wide.region_5.6_spmd, body=%wide.region_4.5_spmd.sunk | while | flops 532485 | bytes 1888407 | solution.py:23
  225.7 1.0 constant_dynamic-slice_fusion.2
  227.3 1.0 constant_dynamic-slice_fusion.2
  229.0 1.0 constant_dynamic-slice_fusion.2
  230.6 1.0 constant_dynamic-slice_fusion.2
  232.3 1.0 constant_dynamic-slice_fusion.2
  234.0 1.0 constant_dynamic-slice_fusion.2
  235.6 1.0 constant_dynamic-slice_fusion.2
  237.7 0.7 gather_fusion.3
  238.4 1.1 broadcast_in_dim.93
  239.5 18.0 %all-to-all-start.1 = ((bf16[32,32,512]{2,1,0:T(8,128)(2,1)}), bf16[32,32,512]{2,1,0:T(8,128)(2,1)S(1)}, u32[]{:S(2)}, u32[]{:S(2)}) async-start(bf16[32,32,512]{2,1,0:T(8,128)(2,1)} %broadcast_in_dim.93), calls=%async_computation.1 | async-start | bytes 2097152 | tf_op jit(solution)/shard_map/all_to_all | solution.py:30
  257.7 0.6 reduce-window.6
  258.3 54.7 %all-to-all-done.1 = bf16[32,32,512]{2,1,0:T(8,128)(2,1)S(1)} async-done(((bf16[32,32,512]{2,1,0:T(8,128)(2,1)}), bf16[32,32,512]{2,1,0:T(8,128)(2,1)S(1)}, u32[]{:S(2)}, u32[]{:S(2)}) %all-to-all-start.1) | async-done | bytes 1048608 | tf_op jit(solution)/shard_map/all_to_all | solution.py:30
  313.0 0.4 convolution_convert_fusion.2
  313.9 4.2 all_to_all.45
  318.3 0.9 reshape.320
  319.2 4.0 all-to-all-start.3
  323.6 11.5 %all-to-all-done.3 = bf16[16,2,2048]{2,1,0:T(2,128)(2,1)S(1)} async-done(((bf16[16,2,2048]{2,1,0:T(2,128)(2,1)}), bf16[16,2,2048]{2,1,0:T(2,128)(2,1)S(1)}, u32[]{:S(2)}, u32[]{:S(2)}) %all-to-all-start.3) | async-done | bytes 131104 | tf_op jit(solution)/shard_map/all_to_all | solution.py:54
  335.6 0.7 copy.97
  336.3 4.0 all-to-all-start.4
  340.5 7.8 %all-to-all-done.4 = bf16[8,32,256]{2,1,0:T(8,128)(2,1)S(1)} async-done(((bf16[8,32,256]{2,1,0:T(8,128)(2,1)}), bf16[8,32,256]{2,1,0:T(8,128)(2,1)S(1)}, u32[]{:S(2)}, u32[]{:S(2)}) %all-to-all-start.4) | async-done | bytes 131104 | tf_op jit(solution)/shard_map/all_to_all | solution.py:66
  348.4 0.7 add_convert_fusion.1
  349.1 2.2 scatter_custom_fusion
  351.6 27.2 %all_to_all.46 = bf16[32,2,6,256]{3,1,2,0:T(2,128)(2,1)S(1)} all-to-all(bf16[32,2,6,256]{3,1,2,0:T(2,128)(2,1)S(1)} %copy.103), channel_id=1, replica_groups=mesh['groups'=2,'expert_0'=16,'expert_1'=2,'tensor'=8] {'expert_0','expe..., dimensions={0} | all-to-all | bytes 393216 | tf_op jit(solution)/shard_map/all_to_all | solution.py:202
  379.0 40.4 %all_to_all.47 = bf16[8,32,2,6,256]{4,1,3,2,0:T(8,128)(2,1)S(1)} all-to-all(bf16[8,32,2,6,256]{4,1,3,2,0:T(8,128)(2,1)S(1)} %broadcast_in_dim.95), channel_id=1, replica_groups=mesh['groups'=2,'expert_0'=16,'expert_1'=2,'tensor'=8] {'tensor'}, dimensions={0} | all-to-all | bytes 3145728 | tf_op jit(solution)/shard_map/all_to_all | solution.py:30
  419.6 1.0 copy-done.5
  420.6 0.6 convolution_bitcast_fusion.2
  421.2 3.4 convolution_convert_fusion
  424.6 1.6 copy.148
  426.2 40.0 %all_to_all.48 = bf16[8,32,2,6,256]{4,1,3,2,0:T(8,128)(2,1)S(1)} all-to-all(bf16[8,32,2,6,256]{4,1,3,2,0:T(8,128)(2,1)S(1)} %bitcast.145), channel_id=1, replica_groups=mesh['groups'=2,'expert_0'=16,'expert_1'=2,'tensor'=8] {'tensor'}, dimensions={0} | all-to-all | bytes 3145728 | tf_op jit(solution)/shard_map/all_to_all | solution.py:66
  466.5 0.9 copy.108
  467.4 9.0 %all-to-all-start.8 = ((bf16[32,2,6,256]{3,1,2,0:T(2,128)(2,1)}), bf16[32,2,6,256]{3,1,2,0:T(2,128)(2,1)S(1)}, u32[]{:S(2)}, u32[]{:S(2)}) async-start(bf16[32,2,6,256]{3,1,2,0:T(2,128)(2,1)} %copy.108), calls=%async_computation.8 | async-start | bytes 393216 | tf_op jit(solution)/shard_map/all_to_all | solution.py:211
  476.5 18.4 %all-to-all-done.8 = bf16[32,2,6,256]{3,1,2,0:T(2,128)(2,1)S(1)} async-done(((bf16[32,2,6,256]{3,1,2,0:T(2,128)(2,1)}), bf16[32,2,6,256]{3,1,2,0:T(2,128)(2,1)S(1)}, u32[]{:S(2)}, u32[]{:S(2)}) %all-to-all-start.8) | async-done | bytes 196640 | tf_op jit(solution)/shard_map/all_to_all | solution.py:211
  495.0 1.2 gather_fusion.4
  496.3 0.6 add_convert_fusion
  (115 shorter events, 10.3 us)
Async XLA Ops:
  6.5 414.7 %copy-start = (bf16[2,128,2048]{2,1,0:T(8,128)(2,1)S(1)}, bf16[2,128,2048]{2,1,0:T(8,128)(2,1)}, u32[]{:S(2)}) copy-start(bf16[2,128,2048]{2,1,0:T(8,128)(2,1)} %param.25) | copy-start | bytes 3145732
  9.1 45.6 %copy-start.1 = (s32[32]{0:T(128)S(1)}, s32[32]{0:T(128)}, u32[]{:S(2)}) copy-start(s32[32]{0:T(128)} %param.18) | copy-start | bytes 388
  9.1 49.5 %copy-start.2 = (bf16[32,4096]{1,0:T(8,128)(2,1)S(1)}, bf16[32,4096]{1,0:T(8,128)(2,1)}, u32[]{:S(2)}) copy-start(bf16[32,4096]{1,0:T(8,128)(2,1)} %param.14) | copy-start | bytes 786436
  9.1 151.2 %all-to-all-start = ((bf16[32,1,32,1024]{3,2,1,0:T(8,128)(2,1)}), bf16[32,1,32,1024]{3,2,1,0:T(8,128)(2,1)S(1)}, u32[]{:S(2)}, u32[]{:S(2)}) async-start(bf16[32,1,32,1024]{3,2,1,0:T(8,128)(2,1)} %stack.2), calls=%async_computation | async-start | bytes 4194304 | tf_op jit(solution)/shard_map/all_to_all | solution.py:133
  54.6 169.9 %all-gather.5.cloned.1.call-start = ((), (), s32[]{:S(2)}) async-start(), calls=%async_computation.9 | async-start | bytes 2359296 | tf_op jit(solution)/shard_map/all_gather | solution.py:15
  58.6 3.2 copy-start.3
  62.4 3.3 copy-start.6
  165.1 1.4 copy-start.4
  238.4 19.1 %copy-start.8 = (s32[32,8]{0,1:T(8,128)S(1)}, s32[32,8]{0,1:T(8,128)}, u32[]{:S(2)}) copy-start(s32[32,8]{0,1:T(8,128)} %param.21) | copy-start | bytes 3076
  238.4 74.6 %copy-start.7 = (bf16[512,64]{0,1:T(8,128)(2,1)S(1)}, bf16[512,64]{0,1:T(8,128)(2,1)}, u32[]{:S(2)}) copy-start(bf16[512,64]{0,1:T(8,128)(2,1)} %param.20) | copy-start | bytes 196612
  239.5 73.5 %all-to-all-start.1 = ((bf16[32,32,512]{2,1,0:T(8,128)(2,1)}), bf16[32,32,512]{2,1,0:T(8,128)(2,1)S(1)}, u32[]{:S(2)}, u32[]{:S(2)}) async-start(bf16[32,32,512]{2,1,0:T(8,128)(2,1)} %broadcast_in_dim.93), calls=%async_computation.1 | async-start | bytes 2097152 | tf_op jit(solution)/shard_map/all_to_all | solution.py:30
  319.2 15.9 %all-to-all-start.3 = ((bf16[16,2,2048]{2,1,0:T(2,128)(2,1)}), bf16[16,2,2048]{2,1,0:T(2,128)(2,1)S(1)}, u32[]{:S(2)}, u32[]{:S(2)}) async-start(bf16[16,2,2048]{2,1,0:T(2,128)(2,1)} %reshape.320), calls=%async_computation.3 | async-start | bytes 262144 | tf_op jit(solution)/shard_map/all_to_all | solution.py:54
  336.3 12.1 %all-to-all-start.4 = ((bf16[8,32,256]{2,1,0:T(8,128)(2,1)}), bf16[8,32,256]{2,1,0:T(8,128)(2,1)S(1)}, u32[]{:S(2)}, u32[]{:S(2)}) async-start(bf16[8,32,256]{2,1,0:T(8,128)(2,1)} %copy.97), calls=%async_computation.4 | async-start | bytes 262144 | tf_op jit(solution)/shard_map/all_to_all | solution.py:66
  419.4 1.2 copy-start.5
  466.2 10.2 %copy-start.9 = (f32[32,8]{0,1:T(8,128)S(1)}, f32[32,8]{0,1:T(8,128)}, u32[]{:S(2)}) copy-start(f32[32,8]{0,1:T(8,128)} %param.22) | copy-start | bytes 3076
  467.4 27.5 %all-to-all-start.8 = ((bf16[32,2,6,256]{3,1,2,0:T(2,128)(2,1)}), bf16[32,2,6,256]{3,1,2,0:T(2,128)(2,1)S(1)}, u32[]{:S(2)}, u32[]{:S(2)}) async-start(bf16[32,2,6,256]{3,1,2,0:T(2,128)(2,1)} %copy.108), calls=%async_computation.8 | async-start | bytes 393216 | tf_op jit(solution)/shard_map/all_to_all | solution.py:211
Sparse Core Ops, SparseCore 0:
  170.8 53.5 all-gather.4
